TPU v7x, 256 devices: a whole 4x4x8 slice. The times are simulated.
256 devices in a mesh: lon: 64 (over y, z, x_hi), lat: 4 (over x_lo, core).
Axes of the slice: x: 4 (x_hi: 2, x_lo: 2; x = x_hi * 2 + x_lo), y: 4, z: 8, core: 2. Of those that a mesh axis runs over, the one named last changes fastest.
Arguments:
- terrain_relief: float32 [1, 21504, 10752], P(None, 'lon', 'lat'), may hold values from -30 to 30
Outputs:
- smoothed: float32 [1, 21504, 10752], P(None, 'lon', 'lat')
- slope: float32 [1, 21504, 10752], P(None, 'lon', 'lat')
All inputs are finite; a program needn't handle non-finite values.
Results may differ from a plain program's by a relative error of at most 0.0001.
Values sent between devices are 32-bit elements; how exact they have to be, the bound alone decides.
A program may use at most 64 MiB of HBM per device.

v0:
```python
import jax
import jax.numpy as jnp
from jax import lax
from jax.sharding import PartitionSpec as P


def with_halo(cells, sides, width):
    for axis, dim in sides:
        count = lax.axis_size(axis)
        head = lax.slice_in_dim(cells, 0, width, axis=dim)
        tail = lax.slice_in_dim(cells, cells.shape[dim] - width, cells.shape[dim], axis=dim)
        cells = jnp.concatenate(
            [
                lax.ppermute(tail, axis, [(i, (i + 1) % count) for i in range(count)]),
                cells,
                lax.ppermute(head, axis, [((i + 1) % count, i) for i in range(count)]),
            ],
            axis=dim,
        )
    return cells


def copy_for_each(shard, axis):
    copies = jnp.broadcast_to(shard, (lax.axis_size(axis), *shard.shape))
    return lax.all_to_all(copies, axis, split_axis=0, concat_axis=0, tiled=True)


def over_copies(shard, axis):
    everything = copy_for_each(shard, axis)
    return jnp.sum(everything, axis=0)


def together(arrays, axis):
    flat, at, done = (jnp.concatenate([a.reshape(-1) for a in arrays]), 0, [])
    running = over_copies(flat, axis)
    for a in arrays:
        done.append(running[at : at + a.size].reshape(a.shape))
        at += a.size
    return tuple(done)


def extend(relief_surface, width, first_row, total_rows):
    grown = with_halo(relief_surface, (("lon", 1), ("lat", 2)), width)
    global_rows = first_row - width + jnp.arange(grown.shape[2], dtype=jnp.int32)
    inside = (global_rows >= 0) & (global_rows < total_rows)
    return jnp.where(inside, grown, 0.0)


def box_mean(extended, first_row, total_rows):
    col_span = extended.shape[1] - 4
    row_span = extended.shape[2] - 4
    lon_sum = sum((extended[:, offset : offset + col_span, :] for offset in range(5)))
    box_total = sum((lon_sum[:, :, offset : offset + row_span] for offset in range(5)))
    global_rows = first_row + 2 + jnp.arange(row_span, dtype=jnp.int32)
    counted = jnp.maximum(
        jnp.minimum(global_rows + 2, total_rows - 1) - jnp.maximum(global_rows - 2, 0) + 1, 1
    ).astype(jnp.float32)
    inside = (global_rows >= 0) & (global_rows < total_rows)
    return jnp.where(inside, box_total / (5.0 * counted), 0.0)


def polar_restore(relief_surface, first_row, lead, meridian_count, total_rows, total_cols):
    global_rows = first_row + jnp.arange(relief_surface.shape[2], dtype=jnp.int32)
    north = global_rows == 0
    south = global_rows == total_rows - 1
    inner = relief_surface[:, lead : lead + meridian_count, :]
    northern_portion = jnp.sum(jnp.where(north, inner, 0.0), axis=(1, 2))
    south_part = jnp.sum(jnp.where(south, inner, 0.0), axis=(1, 2))
    totals = together((northern_portion, south_part), "lon")
    north_mean = totals[0] / total_cols
    south_mean = totals[1] / total_cols
    relief_surface = jnp.where(north, north_mean[:, None, None], relief_surface)
    return jnp.where(south, south_mean[:, None, None], relief_surface)


def horn_slope(extended, first_row, total_rows):
    across = extended[:, 2:, :] - extended[:, :-2, :]
    east_west = across[:, :, :-2] + 2.0 * across[:, :, 1:-1] + across[:, :, 2:]
    upward = extended[:, :, 2:] - extended[:, :, :-2]
    north_south = upward[:, :-2, :] + 2.0 * upward[:, 1:-1, :] + upward[:, 2:, :]
    parallel_count = east_west.shape[2]
    global_rows = (first_row + 1 + jnp.arange(parallel_count, dtype=jnp.int32)).astype(jnp.float32)
    latitude = jnp.pi * ((global_rows + 0.5) / total_rows - 0.5)
    stretch = 1.0 / jnp.maximum(jnp.cos(latitude), 0.1)
    grad_x = east_west * stretch / 8.0
    grad_y = north_south / 8.0
    return jnp.sqrt(1.0 + grad_x * grad_x + grad_y * grad_y)


def local(terrain_relief):
    meridian_count = terrain_relief.shape[1]
    parallel_count = terrain_relief.shape[2]
    total_cols = meridian_count * lax.axis_size("lon")
    total_rows = parallel_count * lax.axis_size("lat")
    band_start = lax.axis_index("lat") * parallel_count
    grown = extend(terrain_relief, 5, band_start, total_rows)
    relief_surface = box_mean(grown, band_start - 5, total_rows)
    relief_surface = polar_restore(
        relief_surface, band_start - 3, 3, meridian_count, total_rows, total_cols
    )
    relief_surface = box_mean(relief_surface, band_start - 3, total_rows)
    relief_surface = polar_restore(
        relief_surface, band_start - 1, 1, meridian_count, total_rows, total_cols
    )
    smoothed = relief_surface[:, 1:-1, 1:-1]
    slope = horn_slope(relief_surface, band_start - 1, total_rows)
    return (smoothed, slope)


def solution(mesh):
    placed = (P(None, "lon", "lat"),)
    return jax.shard_map(
        local,
        mesh=mesh,
        in_specs=placed,
        out_specs=(P(None, "lon", "lat"), P(None, "lon", "lat")),
        check_vma=False,
    )
```

profile of v0, /device:TPU:32, one launch (start us, length us, event | category | flops | bytes accessed | tf_op | source)
XLA Modules:
  0.0 126.9 jit_solution(1304331101165325465)
XLA Ops:
  0.6 0.9 fusion.28
  1.6 2.6 %collective-permute-start.1 = (f32[1,5,2688]{2,1,0:T(8,128)S(1)}, f32[1,5,2688]{2,1,0:T(8,128)S(1)}, u32[]{:S(2)}, u32[]{:S(2)}) collective-permute-start(f32[1,5,2688]{2,1,0:T(8,128)S(1)} %get-tuple-element.9), channel_id=1, source_target_pairs={{4,0},{8,4},{12,8},{16,12},{20,16},{24,20},{28,24},{32,28},{36,32}... | collective-permute-start | bytes 161288 | tf_op jit(solution)/shard_map/ppermute | solution.py:16
  4.2 1.0 collective-permute-start
  5.3 2.4 %collective-permute-done.1 = f32[1,5,2688]{2,1,0:T(8,128)S(1)} collective-permute-done((f32[1,5,2688]{2,1,0:T(8,128)S(1)}, f32[1,5,2688]{2,1,0:T(8,128)S(1)}, u32[]{:S(2)}, u32[]{:S(2)}) %collective-permute-start.1) | collective-permute-done | bytes 53792 | tf_op jit(solution)/shard_map/ppermute | solution.py:16
  7.6 3.5 %collective-permute-done = f32[1,5,2688]{2,1,0:T(8,128)S(1)} collective-permute-done((f32[1,5,2688]{2,1,0:T(8,128)S(1)}, f32[1,5,2688]{2,1,0:T(8,128)S(1)}, u32[]{:S(2)}, u32[]{:S(2)}) %collective-permute-start) | collective-permute-done | bytes 53792 | tf_op jit(solution)/shard_map/ppermute | solution.py:14
  11.1 2.3 %pad_maximum_fusion = f32[1,346,2688]{2,1,0:T(8,128)S(1)} fusion(f32[1,5,2688]{2,1,0:T(8,128)S(1)} %collective-permute-done.1, f32[1,336,2688]{2,1,0:T(8,128)} %param.1, f32[1,5,2688]{2,1,0:T(8,128)S(1)} %collective-permute-done), kind=kLoop, calls=%fused_computation.23 | loop fusion | flops 1860096 | bytes 7440384 | tf_op jit(solution)/shard_map/concatenate | solution.py:12
  13.4 0.0 copy-start.2
  13.4 1.9 %copy-done.2 = f32[1,346,2688]{2,1,0:T(8,128)} copy-done((f32[1,346,2688]{2,1,0:T(8,128)}, f32[1,346,2688]{2,1,0:T(8,128)S(1)}, u32[]{:S(2)}) %copy-start.2) | copy-done | bytes 3720216
  15.3 0.1 fusion.27
  15.4 0.1 collective-permute-start.2
  15.5 1.7 %collective-permute-start.3 = (f32[1,346,5]{2,1,0:T(8,128)S(1)}, f32[1,346,5]{2,1,0:T(8,128)S(1)}, u32[]{:S(2)}, u32[]{:S(2)}) collective-permute-start(f32[1,346,5]{2,1,0:T(8,128)S(1)} %get-tuple-element.6), channel_id=1, source_target_pairs={{1,0},{2,1},{3,2},{0,3},{5,4},{6,5},{7,6},{4,7},{9,8},{10,9},{11,1... | collective-permute-start | bytes 20768 | tf_op jit(solution)/shard_map/ppermute | solution.py:16
  17.2 4.2 %collective-permute-done.2 = f32[1,346,5]{2,1,0:T(8,128)S(1)} collective-permute-done((f32[1,346,5]{2,1,0:T(8,128)S(1)}, f32[1,346,5]{2,1,0:T(8,128)S(1)}, u32[]{:S(2)}, u32[]{:S(2)}) %collective-permute-start.2) | collective-permute-done | bytes 6952 | tf_op jit(solution)/shard_map/ppermute | solution.py:14
  21.4 0.0 collective-permute-done.3
  21.4 5.1 %concatenate.21 = f32[1,346,2698]{2,1,0:T(8,128)} concatenate(f32[1,346,5]{2,1,0:T(8,128)S(1)} %collective-permute-done.2, f32[1,346,2688]{2,1,0:T(8,128)} %copy-done.2, f32[1,346,5]{2,1,0:T(8,128)S(1)} %collective-permute-done.3), dimensions={2} | concatenate | bytes 7468064 | tf_op jit(solution)/shard_map/concatenate | solution.py:12
  26.6 2.4 %broadcast_select_fusion = f32[1,346,2698]{2,1,0:T(8,128)S(1)} fusion(f32[1,346,2698]{2,1,0:T(8,128)} %concatenate.21, pred[2698]{0:T(1024)(128)(4,1)S(1)} %fusion.26), kind=kLoop, calls=%fused_computation.43 | loop fusion | flops 933508 | bytes 7470762 | tf_op jit(solution)/shard_map/jit(_where)/select_n | solution.py:46
  29.0 1.6 %slice_add_fusion.12 = f32[1,342,2698]{2,1,0:T(8,128)S(1)} fusion(f32[1,346,2698]{2,1,0:T(8,128)S(1)} %broadcast_select_fusion), kind=kLoop, calls=%fused_computation.16 | loop fusion | flops 3690864 | bytes 22145184 | tf_op jit(solution)/shard_map/add | solution.py:52
  30.5 0.0 copy-start.1
  30.5 4.3 %fusion.3 = f32[1,342,2694]{2,1,0:T(8,128)S(1)} fusion(f32[1,342,2698]{2,1,0:T(8,128)S(1)} %slice_add_fusion.12, f32[2694]{0:T(1024)S(1)} %convert_multiply_fusion.1, pred[2694]{0:T(1024)(128)(4,1)S(1)} %fusion.25), kind=kLoop, calls=%fused_computation.12 | loop fusion | flops 5528088 | bytes 22125822 | tf_op jit(solution)/shard_map/jit(_where)/select_n | solution.py:59
  34.8 0.0 copy-done.1
  34.8 1.6 %select_reduce_fusion.3 = (f32[]{:T(128)}, f32[]{:T(128)}) fusion(f32[1,342,2694]{2,1,0:T(8,128)S(1)} %fusion.3, pred[2694]{0:T(1024)(128)(4,1)S(1)} %get-tuple-element.14, pred[2694]{0:T(1024)(128)(4,1)S(1)} %get-tuple-element.15), kind=kLoop, calls=%fused_computation.27 | loop fusion | flops 3620734 | bytes 3626132 | tf_op jit(solution)/shard_map/reduce_sum | solution.py:67
  36.4 1.4 %pad_maximum_fusion.1 = f32[2]{0:T(128)S(1)} fusion(f32[1]{0:T(128)} %bitcast.1, f32[1]{0:T(128)} %bitcast), kind=kLoop, calls=%fused_computation.63 | loop fusion | flops 2 | bytes 16 | tf_op jit(solution)/shard_map/concatenate | solution.py:34
  37.8 0.6 broadcast_in_dim.120
  38.5 15.7 %all-to-all-start = ((f32[64,1,2]{2,1,0:T(1,128)}), f32[64,1,2]{2,1,0:T(1,128)S(1)}, u32[]{:S(2)}, u32[]{:S(2)}) async-start(f32[64,1,2]{2,1,0:T(1,128)} %broadcast_in_dim.120), calls=%async_computation | async-start | bytes 65536 | tf_op jit(solution)/shard_map/all_to_all | solution.py:25
  54.1 11.1 %all-to-all-done = f32[64,1,2]{2,1,0:T(1,128)S(1)} async-done(((f32[64,1,2]{2,1,0:T(1,128)}), f32[64,1,2]{2,1,0:T(1,128)S(1)}, u32[]{:S(2)}, u32[]{:S(2)}) %all-to-all-start) | async-done | bytes 544 | tf_op jit(solution)/shard_map/all_to_all | solution.py:25
  65.2 0.1 reduce_sum.66
  65.3 0.6 fusion.30
  67.2 11.6 %select_select_fusion.1 = f32[1,342,2694]{2,1,0:T(8,128)S(1)} fusion(f32[]{:T(128)} %bitcast.3, f32[]{:T(128)} %bitcast.2, pred[2694]{0:T(1024)(128)(4,1)S(1)} %get-tuple-element.14, pred[2694]{0:T(1024)(128)(4,1)S(1)} %get-tuple-element.15, f32[2694]{0:T(1024)S(1)} %convert_multiply_fusion.1, f32[1,342,2698]{2,1,0:T(8,128)} %copy-done.1, ...), kind=kLoop, calls=%fused_computation.21 | loop fusion | flops 7370784 | bytes 22131218 | tf_op jit(solution)/shard_map/jit(_where)/select_n | solution.py:73
  78.8 1.6 %slice_add_fusion.4 = f32[1,338,2694]{2,1,0:T(8,128)S(1)} fusion(f32[1,342,2694]{2,1,0:T(8,128)S(1)} %select_select_fusion.1), kind=kLoop, calls=%fused_computation.6 | loop fusion | flops 3642288 | bytes 21853728 | tf_op jit(solution)/shard_map/add | solution.py:52
  80.3 0.0 copy-start
  80.4 4.3 %fusion.1 = f32[1,338,2690]{2,1,0:T(8,128)S(1)} fusion(f32[1,338,2694]{2,1,0:T(8,128)S(1)} %slice_add_fusion.4, f32[2690]{0:T(1024)S(1)} %convert_multiply_fusion, pred[2690]{0:T(1024)(128)(4,1)S(1)} %fusion.24), kind=kLoop, calls=%fused_computation.2 | loop fusion | flops 5455320 | bytes 21834730 | tf_op jit(solution)/shard_map/jit(_where)/select_n | solution.py:59
  84.6 0.0 copy-done
  84.6 1.6 %select_reduce_fusion.1 = (f32[]{:T(128)}, f32[]{:T(128)}) fusion(f32[1,338,2690]{2,1,0:T(8,128)S(1)} %fusion.1, pred[2690]{0:T(1024)(128)(4,1)S(1)} %get-tuple-element.16, pred[2690]{0:T(1024)(128)(4,1)S(1)} %get-tuple-element.17), kind=kLoop, calls=%fused_computation.25 | loop fusion | flops 3615358 | bytes 3620748 | tf_op jit(solution)/shard_map/reduce_sum | solution.py:67
  86.3 1.4 %pad_maximum_fusion.2 = f32[2]{0:T(128)S(1)} fusion(f32[1]{0:T(128)} %bitcast.5, f32[1]{0:T(128)} %bitcast.4), kind=kLoop, calls=%fused_computation.64 | loop fusion | flops 2 | bytes 16 | tf_op jit(solution)/shard_map/concatenate | solution.py:34
  87.6 0.6 broadcast_in_dim.129
  88.3 5.4 %all-to-all-start.1 = ((f32[64,1,2]{2,1,0:T(1,128)}), f32[64,1,2]{2,1,0:T(1,128)S(1)}, u32[]{:S(2)}, u32[]{:S(2)}) async-start(f32[64,1,2]{2,1,0:T(1,128)} %broadcast_in_dim.129), calls=%async_computation.1 | async-start | bytes 65536 | tf_op jit(solution)/shard_map/all_to_all | solution.py:25
  93.7 0.1 maximum_divide_fusion
  93.7 10.9 %all-to-all-done.1 = f32[64,1,2]{2,1,0:T(1,128)S(1)} async-done(((f32[64,1,2]{2,1,0:T(1,128)}), f32[64,1,2]{2,1,0:T(1,128)S(1)}, u32[]{:S(2)}, u32[]{:S(2)}) %all-to-all-start.1) | async-done | bytes 544 | tf_op jit(solution)/shard_map/all_to_all | solution.py:25
  104.7 0.1 reduce_sum.71
  104.8 0.6 fusion.29
  106.7 11.6 %select_select_fusion = f32[1,338,2690]{2,1,0:T(8,128)S(1)} fusion(f32[]{:T(128)} %bitcast.7, f32[]{:T(128)} %bitcast.6, pred[2690]{0:T(1024)(128)(4,1)S(1)} %get-tuple-element.16, pred[2690]{0:T(1024)(128)(4,1)S(1)} %get-tuple-element.17, f32[2690]{0:T(1024)S(1)} %convert_multiply_fusion, f32[1,338,2694]{2,1,0:T(8,128)} %copy-done, ...), kind=kLoop, calls=%fused_computation.20 | loop fusion | flops 7273760 | bytes 21840118 | tf_op jit(solution)/shard_map/jit(_where)/select_n | solution.py:73
  118.3 2.8 %slice.188 = f32[1,336,2688]{2,1,0:T(8,128)} slice(f32[1,338,2690]{2,1,0:T(8,128)S(1)} %select_select_fusion), slice={[0:1], [1:337], [1:2689]} | slice | bytes 7225344 | tf_op jit(solution)/shard_map/slice | solution.py:105
  121.1 1.0 slice_subtract_fusion.1
  122.1 0.4 slice_subtract_fusion
  122.5 4.4 %fusion.7 = f32[1,336,2688]{2,1,0:T(8,128)} fusion(f32[1,338,2688]{2,1,0:T(8,128)S(1)} %slice_subtract_fusion.1, f32[1,336,2690]{2,1,0:T(8,128)S(1)} %slice_subtract_fusion, f32[2688]{0:T(1024)S(1)} %maximum_divide_fusion), kind=kLoop, calls=%fused_computation.33 | loop fusion | flops 11741184 | bytes 25299456 | tf_op jit(solution)/shard_map/sqrt | solution.py:87
  (7 shorter events, 0.1 us)
Async XLA Ops:
  1.6 6.1 %collective-permute-start.1 = (f32[1,5,2688]{2,1,0:T(8,128)S(1)}, f32[1,5,2688]{2,1,0:T(8,128)S(1)}, u32[]{:S(2)}, u32[]{:S(2)}) collective-permute-start(f32[1,5,2688]{2,1,0:T(8,128)S(1)} %get-tuple-element.9), channel_id=1, source_target_pairs={{4,0},{8,4},{12,8},{16,12},{20,16},{24,20},{28,24},{32,28},{36,32}... | collective-permute-start | bytes 161288 | tf_op jit(solution)/shard_map/ppermute | solution.py:16
  4.2 6.9 %collective-permute-start = (f32[1,5,2688]{2,1,0:T(8,128)S(1)}, f32[1,5,2688]{2,1,0:T(8,128)S(1)}, u32[]{:S(2)}, u32[]{:S(2)}) collective-permute-start(f32[1,5,2688]{2,1,0:T(8,128)S(1)} %get-tuple-element.8), channel_id=1, source_target_pairs={{0,4},{4,8},{8,12},{12,16},{16,20},{20,24},{24,28},{28,32},{32,36}... | collective-permute-start | bytes 161288 | tf_op jit(solution)/shard_map/ppermute | solution.py:14
  13.4 1.9 %copy-start.2 = (f32[1,346,2688]{2,1,0:T(8,128)}, f32[1,346,2688]{2,1,0:T(8,128)S(1)}, u32[]{:S(2)}) copy-start(f32[1,346,2688]{2,1,0:T(8,128)S(1)} %pad_maximum_fusion) | copy-start | bytes 11160580
  15.4 6.0 %collective-permute-start.2 = (f32[1,346,5]{2,1,0:T(8,128)S(1)}, f32[1,346,5]{2,1,0:T(8,128)S(1)}, u32[]{:S(2)}, u32[]{:S(2)}) collective-permute-start(f32[1,346,5]{2,1,0:T(8,128)S(1)} %get-tuple-element.7), channel_id=1, source_target_pairs={{0,1},{1,2},{2,3},{3,0},{4,5},{5,6},{6,7},{7,4},{8,9},{9,10},{10,1... | collective-permute-start | bytes 20768 | tf_op jit(solution)/shard_map/ppermute | solution.py:14
  15.5 6.0 %collective-permute-start.3 = (f32[1,346,5]{2,1,0:T(8,128)S(1)}, f32[1,346,5]{2,1,0:T(8,128)S(1)}, u32[]{:S(2)}, u32[]{:S(2)}) collective-permute-start(f32[1,346,5]{2,1,0:T(8,128)S(1)} %get-tuple-element.6), channel_id=1, source_target_pairs={{1,0},{2,1},{3,2},{0,3},{5,4},{6,5},{7,6},{4,7},{9,8},{10,9},{11,1... | collective-permute-start | bytes 20768 | tf_op jit(solution)/shard_map/ppermute | solution.py:16
  30.5 4.3 %copy-start.1 = (f32[1,342,2698]{2,1,0:T(8,128)}, f32[1,342,2698]{2,1,0:T(8,128)S(1)}, u32[]{:S(2)}) copy-start(f32[1,342,2698]{2,1,0:T(8,128)S(1)} %slice_add_fusion.12) | copy-start | bytes 11072596
  38.5 26.8 %all-to-all-start = ((f32[64,1,2]{2,1,0:T(1,128)}), f32[64,1,2]{2,1,0:T(1,128)S(1)}, u32[]{:S(2)}, u32[]{:S(2)}) async-start(f32[64,1,2]{2,1,0:T(1,128)} %broadcast_in_dim.120), calls=%async_computation | async-start | bytes 65536 | tf_op jit(solution)/shard_map/all_to_all | solution.py:25
  80.3 4.3 %copy-start = (f32[1,338,2694]{2,1,0:T(8,128)}, f32[1,338,2694]{2,1,0:T(8,128)S(1)}, u32[]{:S(2)}) copy-start(f32[1,338,2694]{2,1,0:T(8,128)S(1)} %slice_add_fusion.4) | copy-start | bytes 10926868
  88.3 16.4 %all-to-all-start.1 = ((f32[64,1,2]{2,1,0:T(1,128)}), f32[64,1,2]{2,1,0:T(1,128)S(1)}, u32[]{:S(2)}, u32[]{:S(2)}) async-start(f32[64,1,2]{2,1,0:T(1,128)} %broadcast_in_dim.129), calls=%async_computation.1 | async-start | bytes 65536 | tf_op jit(solution)/shard_map/all_to_all | solution.py:25
where the time goes:
time: 128 us; the launch traced here: 127 us
  other arithmetic  51.6 us (40%)
  waiting for transfers between devices  32.1 us (25%)
  starting transfers between devices  26.5 us (21%)
  local copies, waits for them, and re-layouts  13.3 us (10%)
  between operations  3.43 us (3%)
    select_n x2, other arithmetic, polar_restore(): return jnp.where(south, south_mean[:, None, None], relief_surface)  23.2 us
    all_to_all x2, waiting for transfers between devices, copy_for_each(): return lax.all_to_all(copies, axis, split_axis=0, concat_axis=0, tiled=True)  22 us
    all_to_all x2, starting transfers between devices, copy_for_each(): return lax.all_to_all(copies, axis, split_axis=0, concat_axis=0, tiled=True)  21.1 us
    select_n x2, other arithmetic, box_mean(): return jnp.where(inside, box_total / (5.0 * counted), 0.0)  8.53 us
    ppermute x2, waiting for transfers between devices, with_halo(): lax.ppermute(tail, axis, [(i, (i + 1) % count) for i in range(count)])  7.67 us
    concatenate x1, local copies, waits for them, and re-layouts, with_halo(): jnp.concatenate([lax.ppermute(tail, axis, [(i, (i + 1) % count) for i in...  5.15 us
    sqrt x1, other arithmetic, horn_slope(): return jnp.sqrt(1.0 + grad_x * grad_x + grad_y * grad_y)  4.38 us
    ppermute x2, starting transfers between devices, with_halo(): lax.ppermute(head, axis, [((i + 1) % count, i) for i in range(count)])  4.38 us
  transfers between devices with their start and end apart: 6, of which 5 were waited for; matrix products, arithmetic and copies ran while one was open for 0% of the time, Pallas kernels for 0%

commit v1 on v0

v1 whole, which is shorter than its diff:
```python
import functools
import math

import jax
import jax.numpy as jnp
import numpy as np
from jax import lax
from jax.experimental import pallas as pl
from jax.experimental.pallas import tpu as pltpu
from jax.sharding import PartitionSpec as P

MESH = pl.DeviceIdType.MESH
F32, BF16 = jnp.float32, jnp.bfloat16
LANES = 128
TILE = 8
ABOVE = 16
OVER = 24
DEPTH = 8
SCALE = 1.0 / 625.0


def stencils(smooth):
    ahead, behind = np.zeros_like(smooth), np.zeros_like(smooth)
    ahead[:, :-1], behind[:, 1:] = smooth[:, 1:], smooth[:, :-1]
    return np.concatenate([smooth, ahead + 2 * smooth + behind, ahead - behind], axis=1)


def five(width):
    at = np.arange(width)
    return (np.abs(at[:, None] - at[None, :]) <= 2).astype(np.float64)


def inner_weights():
    span = 4 * LANES
    parts = np.split(stencils(five(span) @ five(span)), 3, axis=1)
    return np.concatenate([p[:, LANES : 3 * LANES] for p in parts], axis=1)


def outer_weights(width, n_lat):
    total = width * n_lat
    lane = np.arange(LANES)
    out = []
    for band in range(n_lat):
        row = band * width + np.where(lane < 64, lane - TILE, width + lane - 120)
        near = (row == 1) | (row == total - 2)
        weight = np.where((row > 0) & (row < total - 1), np.where(near, 1 / 20, 1 / 25), 0.0)
        side = lane < 64
        box = five(LANES) * (side[:, None] == side[None, :])
        smooth = (box * weight[None, :]) @ (box * weight[None, :])
        ahead, behind = np.zeros_like(smooth), np.zeros_like(smooth)
        ahead[:, :-1], behind[:, 1:] = smooth[:, 1:], smooth[:, :-1]
        ahead[:, 63], behind[:, 64] = 0, 0
        out.append(np.concatenate([smooth, ahead + 2 * smooth + behind, ahead - behind], axis=1) / SCALE)
    return np.stack(out)


def column_sum(x, block, row):
    rows = [x[block, pl.ds(row + k, TILE), :] for k in range(-4, 5)]
    s = rows[4]
    value = s
    for k in range(1, 5):
        s = s + (rows[4 - k] + rows[4 + k])
        value = value + s
    return value * SCALE


def halves(value):
    high = value.astype(BF16)
    return high, (value - high.astype(F32)).astype(BF16)


def secant(east, before, middle, after):
    north = before + (middle + middle) + after
    square = 1.0 + east * east + (north * north) * (1.0 / 64.0)
    return square * lax.rsqrt(square)


def stretch_of(row, total):
    latitude = math.pi * ((row.astype(F32) + 0.5) / total - 0.5)
    return 0.125 / jnp.maximum(jnp.cos(latitude), 0.1)


def exchange(
    height, width, n_lon, n_lat, x, w_hbm, outer_high_hbm, outer_low_hbm, z, s,
    xb, vh, vl, q, d, ze, se, stretch, w, outer_high, outer_low, packed, landed, land_rows, corners,
    strip_high, strip_low, part, heard,
    block_sem, weight_sem, send, recv, polar_send, polar_recv,
):
    blocks = width // LANES
    tiles = height // TILE
    total = width * n_lat
    me, band = lax.axis_index("lon"), lax.axis_index("lat")
    up, down = lax.rem(me + 1, n_lon), lax.rem(me + n_lon - 1, n_lon)
    has_left, has_right = band > 0, band < n_lat - 1
    polar = (band == 0) | (band == n_lat - 1)

    depth = min(DEPTH, n_lon // 2)
    plane = n_lon // depth
    high = lax.rem(me, 2)
    deep = lax.rem(lax.div(me, 2), depth)
    broad = lax.div(me, 2 * depth)
    along, across = [], []
    for k in range(1, depth):
        along.append((broad * depth + lax.rem(deep + k, depth)) * 2 + high)
    for k in range(1, plane):
        other = lax.rem(broad * 2 + high + k, plane)
        across.append((lax.div(other, 2) * depth + deep) * 2 + lax.rem(other, 2))

    barrier = pltpu.get_barrier_semaphore()

    def greet(lon, lat):
        pl.semaphore_signal(barrier, inc=1, device_id=(lon, lat), device_id_type=MESH)

    for lon in (up, down):
        greet(lon, band)

    @pl.when(has_left)
    def _():
        for lon in (me, up, down):
            greet(lon, band - 1)

    @pl.when(has_right)
    def _():
        for lon in (me, up, down):
            greet(lon, band + 1)

    @pl.when(polar)
    def _():
        for lon in (*along, *across):
            greet(lon, band)

    def column(b):
        at = pl.ds(pl.multiple_of((b - 1) * LANES, LANES), LANES)
        return pltpu.make_async_copy(x.at[:, at], xb.at[b, pl.ds(OVER, height), :], block_sem.at[b - 1])

    for b in (1, blocks, *range(2, blocks)):
        column(b).start()
    weights = [
        pltpu.make_async_copy(w_hbm, w, weight_sem.at[0]),
        pltpu.make_async_copy(outer_high_hbm.at[band], outer_high, weight_sem.at[1]),
        pltpu.make_async_copy(outer_low_hbm.at[band], outer_low, weight_sem.at[2]),
    ]
    for copy in weights:
        copy.start()

    shape = stretch.shape
    tile_row = lax.broadcasted_iota(jnp.int32, shape, 0)
    tile_lane = lax.broadcasted_iota(jnp.int32, shape, 1)
    inside = (tile_row - 1) * LANES + tile_lane
    side_by_side = jnp.where(tile_lane < 64, tile_lane - TILE, width + tile_lane - 120)
    stretch[...] = stretch_of(band * width + jnp.where(tile_row == 0, side_by_side, inside), total)
    for b in (0, blocks + 1):
        for array in (vh, vl):
            array[:, LANES * b : LANES * b + LANES] = jnp.zeros((array.shape[0], LANES), BF16)
    for array in (strip_high, strip_low):
        array[0, :, 0:LANES] = jnp.zeros((32, LANES), BF16)
        array[blocks // 2, :, 3 * LANES : 4 * LANES] = jnp.zeros((32, LANES), BF16)

    lane = lax.broadcasted_iota(jnp.int32, (TILE, LANES), 1)
    group = lax.shift_right_logical(lane, 3)
    column(1).wait()
    column(blocks).wait()
    for side, b in ((0, 1), (1, blocks)):
        for first in range(0, tiles, 16):
            acc = jnp.zeros((TILE, LANES), F32)
            for t in range(first, min(first + 16, tiles)):
                k = t - first
                tile = xb[b, OVER + TILE * t : OVER + TILE * t + TILE, :]
                shift = (TILE * k + TILE * side) % LANES
                acc = jnp.where(group == k, pltpu.roll(tile, shift, 1) if shift else tile, acc)
            packed[side, first // 2 : first // 2 + TILE, :] = acc

    @pl.when(polar)
    def _():
        b = jnp.where(band == 0, 1, blocks)
        sums = [xb[b, OVER + TILE * t : OVER + TILE * t + TILE, :] for t in range(tiles)]
        while len(sums) > 1:
            sums = [p + r for p, r in zip(sums[::2], sums[1::2])] + ([sums[-1]] if len(sums) % 2 else [])
        part[0] = sums[0]

    def columns(b, carry):
        @pl.when((b > 1) & (b < blocks))
        def _():
            column(b).wait()

        at = pl.ds(pl.multiple_of(b * LANES, LANES), LANES)
        for t in range(height // 16):
            row = 16 * t
            value = jnp.concatenate([column_sum(xb, b, OVER + row + h) for h in (0, TILE)], axis=0)
            vh[ABOVE + row : ABOVE + row + 16, at], vl[ABOVE + row : ABOVE + row + 16, at] = halves(value)
        return carry

    def products(j, carry):
        b = jnp.minimum(1 + 2 * j, blocks - 1)
        window = pl.ds(pl.multiple_of((b - 1) * LANES, LANES), 4 * LANES)
        out = pl.ds(pl.multiple_of((b - 1) * LANES, LANES), 2 * LANES)
        own = pl.ds(ABOVE, height)
        first, second = vh[own, window], vl[own, window]
        for k in range(3):
            weight = w[:, 2 * LANES * k : 2 * LANES * (k + 1)]
            value = jnp.dot(first, weight, preferred_element_type=F32)
            value = value + jnp.dot(second, weight, preferred_element_type=F32)
            if k == 0:
                z[:, out] = value
            else:
                array = (q, d)[k - 1]
                array[b - 1, ABOVE : ABOVE + height, :] = value[:, :LANES]
                array[b, ABOVE : ABOVE + height, :] = value[:, LANES:]
        return carry

    def slopes(i, carry):
        row = pl.multiple_of(i * TILE, TILE)
        at = row + ABOVE
        for b in range(blocks):
            east = (q[b, pl.ds(at + 1, TILE), :] - q[b, pl.ds(at - 1, TILE), :]) * stretch[b + 1 : b + 2, :]
            rows = [d[b, pl.ds(at + k, TILE), :] for k in (-1, 0, 1)]
            s[pl.ds(row, TILE), LANES * b : LANES * b + LANES] = secant(east, *rows)
        return carry

    pairs = blocks // 2 + 1
    early = deep == 0
    columns_done = jnp.where(early, blocks, 0)
    pairs_done = jnp.where(early, pairs, 0)
    lax.fori_loop(1, 1 + columns_done, columns, 0)
    weights[0].wait()
    lax.fori_loop(0, pairs_done, products, 0)

    @pl.when(polar)
    def _():
        pl.semaphore_wait(barrier, 5 + len(along) + len(across))

    @pl.when(jnp.logical_not(polar))
    def _():
        pl.semaphore_wait(barrier, 8)

    def remote(src, dst, k, lon, lat):
        return pltpu.make_async_remote_copy(
            src, dst, send.at[k], recv.at[k], device_id=(lon, lat), device_id_type=MESH
        )

    head, tail = pl.ds(0, TILE), pl.ds(height - TILE, TILE)
    west, east = pl.ds(0, LANES), pl.ds(width - LANES, LANES)
    rows = [
        remote(x.at[tail, :], land_rows.at[0], 0, up, band),
        remote(x.at[head, :], land_rows.at[1], 1, down, band),
    ]
    to_left = [
        remote(packed.at[0], landed.at[1], 2, me, band - 1),
        remote(x.at[tail, west], corners.at[2], 3, up, band - 1),
        remote(x.at[head, west], corners.at[3], 4, down, band - 1),
    ]
    to_right = [
        remote(packed.at[1], landed.at[0], 5, me, band + 1),
        remote(x.at[tail, east], corners.at[0], 6, up, band + 1),
        remote(x.at[head, east], corners.at[1], 7, down, band + 1),
    ]

    def sums(stage, members, first):
        return [
            pltpu.make_async_remote_copy(
                part.at[stage], heard.at[first + k], polar_send.at[first + k], polar_recv.at[first + k],
                device_id=(lon, band), device_id_type=MESH,
            )
            for k, lon in enumerate(members)
        ]

    first_sums, second_sums = sums(0, along, 0), sums(1, across, len(along))

    @pl.when(polar)
    def _():
        for copy in first_sums:
            copy.start()

    for copy in rows:
        copy.start()

    @pl.when(has_left)
    def _():
        for copy in to_left:
            copy.start()

    @pl.when(has_right)
    def _():
        for copy in to_right:
            copy.start()

    lax.fori_loop(1 + columns_done, 1 + blocks, columns, 0)
    pairs_half = jnp.where(early, pairs, pairs // 2)
    lax.fori_loop(pairs_done, pairs_half, products, 0)

    @pl.when(polar)
    def _():
        for copy in first_sums:
            copy.wait_recv()
        value = part[0]
        for k in range(len(along)):
            value = value + heard[k]
        part[1] = value
        for copy in second_sums:
            copy.start()

    lax.fori_loop(pairs_half, pairs, products, 0)
    lax.fori_loop(0, tiles, slopes, 0)

    def pack(left, mine_left, mine_right, right, row):
        tile = jnp.where(
            lane < TILE, left, jnp.where(lane < 64, mine_left, jnp.where(lane < 120, mine_right, right))
        )
        xb[0, pl.ds(row, TILE), :] = tile

    def own_sides(row):
        return pltpu.roll(xb[1, pl.ds(row, TILE), :], TILE, 1), pltpu.roll(
            xb[blocks, pl.ds(row, TILE), :], LANES - TILE, 1
        )

    for t in range(tiles):
        row = OVER + TILE * t
        xb[0, row : row + TILE, :] = jnp.where(lane < 64, *own_sides(row))

    @pl.when(has_left)
    def _():
        for copy in to_right:
            copy.wait_recv()

    @pl.when(has_right)
    def _():
        for copy in to_left:
            copy.wait_recv()

    for copy in rows:
        copy.wait_recv()
    for end, row in ((0, OVER - TILE), (1, OVER + height)):
        for b in range(1, blocks + 1):
            xb[b, row : row + TILE, :] = land_rows[end, :, LANES * (b - 1) : LANES * b]
    for end, row in ((0, OVER - TILE), (1, OVER + height)):
        xb[0, row : row + TILE, :] = jnp.where(lane < 64, *own_sides(row))
    for side, there in ((0, has_left), (1, has_right)):
        mask = lane < TILE if side == 0 else lane >= LANES - TILE

        @pl.when(there)
        def _():
            for t in range(tiles):
                k = t % 16
                row = OVER + TILE * t
                tile = landed[side, t // 16 * TILE : t // 16 * TILE + TILE, :]
                shift = ((LANES - TILE * k) if side == 0 else (LANES - TILE - TILE * k)) % LANES
                tile = pltpu.roll(tile, shift, 1) if shift else tile
                xb[0, row : row + TILE, :] = jnp.where(mask, tile, xb[0, row : row + TILE, :])
            for end, row in ((0, OVER - TILE), (1, OVER + height)):
                shift = TILE if side == 0 else LANES - TILE
                tile = pltpu.roll(corners[2 * side + end], shift, 1)
                xb[0, row : row + TILE, :] = jnp.where(mask, tile, xb[0, row : row + TILE, :])

        @pl.when(jnp.logical_not(there))
        def _():
            for t in range(-1, tiles + 1):
                row = OVER + TILE * t
                xb[0, row : row + TILE, :] = jnp.where(mask, 0.0, xb[0, row : row + TILE, :])

    def strips(j, carry):
        for k in range(4):
            b = jnp.minimum(1 + 2 * j, blocks - 1) - 1 + k

            @pl.when((b > 0) & (b <= blocks))
            def _():
                for end, row in ((0, OVER - TILE), (1, OVER + height - TILE)):
                    value = jnp.concatenate([column_sum(xb, b, row + h) for h in (0, TILE)], axis=0)
                    at = slice(16 * end, 16 * end + 16)
                    cols = slice(LANES * k, LANES * k + LANES)
                    strip_high[j, at, cols], strip_low[j, at, cols] = halves(value)

        return carry

    lax.fori_loop(0, pairs, strips, 0)
    first = strip_high[...].reshape(pairs * 32, 4 * LANES)
    second = strip_low[...].reshape(pairs * 32, 4 * LANES)
    for k in range(3):
        weight = w[:, 2 * LANES * k : 2 * LANES * (k + 1)]
        value = jnp.dot(first, weight, preferred_element_type=F32)
        value = value + jnp.dot(second, weight, preferred_element_type=F32)
        for j in range(pairs):
            b = min(1 + 2 * j, blocks - 1)
            top, bottom = value[32 * j : 32 * j + 16], value[32 * j + 16 : 32 * j + 32]
            if k == 0:
                z[0:TILE, LANES * (b - 1) : LANES * (b + 1)] = top[TILE:]
                z[height - TILE : height, LANES * (b - 1) : LANES * (b + 1)] = bottom[:TILE]
            else:
                array = (q, d)[k - 1]
                for n in range(2):
                    cols = slice(LANES * n, LANES * n + LANES)
                    array[b - 1 + n, ABOVE - TILE : ABOVE + TILE, :] = top[:, cols]
                    array[b - 1 + n, ABOVE + height - TILE : ABOVE + height + TILE, :] = bottom[:, cols]
    slopes(0, 0)
    slopes(tiles - 1, 0)

    for copy in weights[1:]:
        copy.wait()
    for t in range(vh.shape[0] // 16):
        row = 16 * t
        value = jnp.concatenate([column_sum(xb, 0, OVER - ABOVE + row + h) for h in (0, TILE)], axis=0)
        vh[row : row + 16, 0:LANES], vl[row : row + 16, 0:LANES] = halves(value)
    first, second = vh[:, 0:LANES], vl[:, 0:LANES]
    value = jnp.dot(first, outer_high[...], preferred_element_type=F32)
    value = value + jnp.dot(second, outer_high[...], preferred_element_type=F32)
    value = value + jnp.dot(first, outer_low[...], preferred_element_type=F32)
    for k in range(3):
        ze[k] = value[:, LANES * k : LANES * k + LANES]

    @pl.when(polar)
    def _():
        for copy in second_sums:
            copy.wait_recv()
        value = part[1]
        for k in range(len(along), len(along) + len(across)):
            value = value + heard[k]
        north = band == 0
        away = jnp.where(north, lane, LANES - 1 - lane)
        one = 1.0 / (n_lon * height)
        first = jnp.sum(jnp.where(away < 3, value, 0.0)) * (one / 3.0)
        weights = jnp.where(
            away < 3, (1 / 3 + 1 / 4 + 1 / 5) / 3, jnp.where(away == 3, (1 / 4 + 1 / 5) / 3, 1 / 15)
        )
        second = jnp.sum(jnp.where(away < 5, value * weights, 0.0)) * one
        near, next_ = first * 0.25, first * 0.2
        away = jnp.where(north, lane - TILE, 119 - lane)
        lift = jnp.where(
            away == 0, second, jnp.where(away == 1, near, jnp.where(away == 2, next_, 0.0))
        )
        step = jnp.where(
            away == 0, near,
            jnp.where(
                away == 1, next_ - second,
                jnp.where(away == 2, -near, jnp.where(away == 3, -next_, 0.0)),
            ),
        )
        se[0] = lift
        se[1] = jnp.where(north, step, -step) * 4.0

    @pl.when(jnp.logical_not(polar))
    def _():
        se[0] = jnp.zeros((TILE, LANES), F32)
        se[1] = jnp.zeros((TILE, LANES), F32)

    lift, step = se[0], se[1]
    for t in range(tiles):
        row = TILE * t
        at = ABOVE + row
        east_ = (ze[1, at + 1 : at + 9, :] - ze[1, at - 1 : at + 7, :]) * stretch[0:1, :]
        before, middle, after = (ze[2, at + k : at + k + TILE, :] for k in (-1, 0, 1))
        slope = secant(east_, before + step, middle, after)
        smooth = ze[0, at : at + TILE, :] + lift
        here = slice(row, row + TILE)
        for array, value in ((z, smooth), (s, slope)):
            cols = slice(0, LANES)
            array[here, cols] = jnp.where(lane < TILE, pltpu.roll(value, LANES - TILE, 1), array[here, cols])
            cols = slice(width - LANES, width)
            array[here, cols] = jnp.where(lane < LANES - TILE, array[here, cols], pltpu.roll(value, TILE, 1))

    for copy in rows:
        copy.wait_send()

    @pl.when(has_left)
    def _():
        for copy in to_left:
            copy.wait_send()

    @pl.when(has_right)
    def _():
        for copy in to_right:
            copy.wait_send()

    @pl.when(polar)
    def _():
        for copy in (*first_sums, *second_sums):
            copy.wait_send()


def deliver(z, s, smoothed, slope, sems):
    parts = sems.shape[0] // 2
    span = z.shape[0] // parts
    copies = []
    for k in range(parts):
        at = pl.ds(k * span, span)
        copies.append(pltpu.make_async_copy(z.at[at, :], smoothed.at[at, :], sems.at[2 * k]))
        copies.append(pltpu.make_async_copy(s.at[at, :], slope.at[at, :], sems.at[2 * k + 1]))
    for copy in copies:
        copy.start()
    for copy in copies:
        copy.wait()


def local(n_lon, n_lat, terrain_relief):
    _, height, width = terrain_relief.shape
    blocks, tiles = width // LANES, height // TILE
    pairs = blocks // 2 + 1
    depth = min(DEPTH, n_lon // 2)
    others = depth + n_lon // depth - 2
    dma = pltpu.SemaphoreType.DMA
    outer = outer_weights(width, n_lat).astype(np.float32)
    outer_high = outer.astype(BF16)
    outer_low = (outer - outer_high.astype(np.float32)).astype(BF16)
    inner = inner_weights().astype(BF16)
    z, s = pl.pallas_call(
        functools.partial(exchange, height, width, n_lon, n_lat),
        out_shape=(pltpu.VMEM((height, width), F32), pltpu.VMEM((height, width), F32)),
        in_specs=[pl.BlockSpec(memory_space=pltpu.HBM)] * 4,
        out_specs=(pl.BlockSpec(memory_space=pltpu.VMEM), pl.BlockSpec(memory_space=pltpu.VMEM)),
        scratch_shapes=[
            pltpu.VMEM((blocks + 2, height + 2 * OVER, LANES), F32),
            pltpu.VMEM((height + 2 * ABOVE, width + 2 * LANES), BF16),
            pltpu.VMEM((height + 2 * ABOVE, width + 2 * LANES), BF16),
            pltpu.VMEM((blocks, height + 2 * ABOVE, LANES), F32),
            pltpu.VMEM((blocks, height + 2 * ABOVE, LANES), F32),
            pltpu.VMEM((3, height + 2 * ABOVE, LANES), F32),
            pltpu.VMEM((2, TILE, LANES), F32),
            pltpu.VMEM((-(-(blocks + 2) // TILE) * TILE, LANES), F32),
            pltpu.VMEM(inner.shape, BF16),
            pltpu.VMEM(outer.shape[1:], BF16),
            pltpu.VMEM(outer.shape[1:], BF16),
            pltpu.VMEM((2, -(-tiles // 16) * TILE, LANES), F32),
            pltpu.VMEM((2, -(-tiles // 16) * TILE, LANES), F32),
            pltpu.VMEM((2, TILE, width), F32),
            pltpu.VMEM((4, TILE, LANES), F32),
            pltpu.VMEM((pairs, 32, 4 * LANES), BF16),
            pltpu.VMEM((pairs, 32, 4 * LANES), BF16),
            pltpu.VMEM((2, TILE, LANES), F32),
            pltpu.VMEM((others, TILE, LANES), F32),
            dma((blocks,)),
            dma((3,)),
            dma((8,)),
            dma((8,)),
            dma((others,)),
            dma((others,)),
        ],
        compiler_params=pltpu.CompilerParams(
            collective_id=0, has_side_effects=True, vmem_limit_bytes=67043328 - 2 * 4 * height * width - 300000
        ),
    )(terrain_relief.reshape(height, width), jnp.asarray(inner), jnp.asarray(outer_high), jnp.asarray(outer_low))
    shape = jax.ShapeDtypeStruct((height, width), F32)
    smoothed, slope = pl.pallas_call(
        deliver,
        out_shape=(shape, shape),
        in_specs=[pl.BlockSpec(memory_space=pltpu.VMEM)] * 2,
        out_specs=(pl.BlockSpec(memory_space=pltpu.HBM),) * 2,
        scratch_shapes=[dma((12,))],
        compiler_params=pltpu.CompilerParams(vmem_limit_bytes=28 * 2**20),
    )(z, s)
    return smoothed.reshape(terrain_relief.shape), slope.reshape(terrain_relief.shape)


def solution(mesh):
    placed = P(None, "lon", "lat")
    return jax.shard_map(
        functools.partial(local, mesh.shape["lon"], mesh.shape["lat"]),
        mesh=mesh,
        in_specs=(placed,),
        out_specs=(placed, placed),
        check_vma=False,
    )
```

time: 128 us -> 30.1 us (0.24)
  other arithmetic: 51.6 us -> 0 us
  waiting for transfers between devices: 32.1 us -> 0 us
  Pallas kernels: 0 us -> 29.4 us
  starting transfers between devices: 26.5 us -> 0 us
  local copies, waits for them, and re-layouts: 13.3 us -> 0 us
  between operations: 3.43 us -> 0.64 us
    select_n x5 -> x0, other arithmetic: 34.1 us -> none  [the longest x2 23.2 us: polar_restore(): return jnp.where(south, south_mean[:, None, None], relief_surface)]
    pallas_call x0 -> x2, Pallas kernels: none -> 29.4 us  [the longest x1 26.3 us: local(): pl.pallas_call(functools.partial(exchange, height, width, n_lon, n_lat),...]
    all_to_all x2 -> x0, waiting for transfers between devices: 22 us -> none  [copy_for_each(): return lax.all_to_all(copies, axis, split_axis=0, concat_axis=0, tiled=True)]
    all_to_all x2 -> x0, starting transfers between devices: 21.1 us -> none  [copy_for_each(): return lax.all_to_all(copies, axis, split_axis=0, concat_axis=0, tiled=True)]
    ppermute x4 -> x0, waiting for transfers between devices: 10 us -> none  [the longest x2 7.67 us: with_halo(): lax.ppermute(tail, axis, [(i, (i + 1) % count) for i in range(count)])]
    ppermute x4 -> x0, starting transfers between devices: 5.42 us -> none  [the longest x2 4.38 us: with_halo(): lax.ppermute(head, axis, [((i + 1) % count, i) for i in range(count)])]
    concatenate x1 -> x0, local copies, waits for them, and re-layouts: 5.15 us -> none  [with_halo(): jnp.concatenate([lax.ppermute(tail, axis, [(i, (i + 1) % count) for i in...]
    slice x5 -> x0, local copies, waits for them, and re-layouts: 5.04 us -> none  [the longest x1 2.82 us: local(): smoothed = relief_surface[:, 1:-1, 1:-1]]
  transfers between devices with their start and end apart: 6 -> 0, of which waited for: 5 -> 0; matrix products, arithmetic and copies ran while one was open for 0% -> 0% of each run, Pallas kernels for 0% -> 0%
where the time goes in v1:
time: 30.1 us; the launch traced here: 30 us
  Pallas kernels  29.4 us (98%)
  between operations  0.64 us (2%)
    pallas_call x1, Pallas kernels, local(): pl.pallas_call(functools.partial(exchange, height, width, n_lon, n_lat),...  26.3 us
    pallas_call x1, Pallas kernels, local(): pl.pallas_call(deliver, out_shape=(shape, shape), in_specs=[pl.BlockSpec(...  3.04 us

profile of v1, /device:TPU:32, one launch (start us, length us, event | category | flops | bytes accessed | tf_op | source)
XLA Modules:
  0.0 30.0 jit_solution(3937142068720639076)
XLA Ops:
  0.6 26.3 %shard_map.59 = (f32[336,2688]{1,0:T(8,128)S(1)}, f32[336,2688]{1,0:T(8,128)S(1)}) custom-call(f32[336,2688]{1,0:T(8,128)} %bitcast.3, bf16[512,768]{1,0:T(8,128)(2,1)} %constant.6.clone.w_hbm, bf16[4,128,384]{2,1,0:T(8,128)(2,1)} %constant.7.clone.outer_high_hbm, bf16[4,128,384]{2,1,0:T(8,128)(2,1)} %constant.8.clone.outer_low_hbm), custom_call_target="tpu_custom_call" | custom-call | tf_op jit(solution)/shard_map/pallas_call | solution.py:503
  27.0 3.0 %shard_map.60 = (f32[336,2688]{1,0:T(8,128)}, f32[336,2688]{1,0:T(8,128)}) custom-call(f32[336,2688]{1,0:T(8,128)S(1)} %get-tuple-element.6.z, f32[336,2688]{1,0:T(8,128)S(1)} %get-tuple-element.7.s), custom_call_target="tpu_custom_call" | custom-call | tf_op jit(solution)/shard_map/pallas_call | solution.py:540
